TPU v7x, 32 devices: a whole 2x2x4 slice. The times are simulated.
32 devices in a mesh: outer: 4 (over y, x), inner: 8 (over z, core).
Axes of the slice: x: 2, y: 2, z: 4, core: 2. Of those that a mesh axis runs over, the one named last changes fastest.
Arguments:
- acts: bfloat16 [32, 2, 512, 512], P(('outer', 'inner')), may hold values from -6 to 6
- cotangent: bfloat16 [32, 2, 512, 512], P(('outer', 'inner')), may hold values from -6 to 6
- residual: float32 [32, 2048, 128], P(('outer', 'inner')), may hold values from -0.6 to 0.6
- owner_residual: float32 [32, 256, 128], P(('outer', 'inner')), may hold values from -3 to 3
- in_count: int32 [32, 2, 8], P(('outer', 'inner')), may hold values from 1 to 128, as said below
- in_rank: int32 [32, 2, 2048], P(('outer', 'inner')), may hold values from 0 to 255, as said below
- out_count: int32 [32, 2], P(('outer', 'inner')), may hold values from 1 to 128
- out_rank: int32 [32, 2, 256], P(('outer', 'inner')), may hold values from 0 to 255, as said below
Outputs:
- applied: bfloat16 [512, 512], replicated
- new_residual: float32 [32, 2048, 128], P(('outer', 'inner'))
- new_owner_residual: float32 [32, 256, 128], P(('outer', 'inner'))
Inputs may be any that keep to these rules, and one draw needn't show every extreme that they name: `in_count`: each step has one owner that receives 128 blocks from every replica. `in_rank`: for each replica, step and owner, the ranks of that owner's 256 blocks are a permutation of 0 to 255. `out_rank`: for each replica and step a permutation of 0 to 255.
All inputs are finite; a program needn't handle non-finite values.
Results may differ from a plain program's by a relative error of at most 0.0065.
Values may be sent and summed in bfloat16 or wider, within the bound.
A program may use at most 64 MiB of HBM per device.

v0:
```python
import math
import jax
import jax.numpy as jnp
from jax import lax
from jax.sharding import PartitionSpec as P

step_size = 0.0625


def select_blocks(resid, grad, ranks_flat, counts, owners, region, width):
    blocks = resid.shape[0]
    accum = (resid + grad.reshape(blocks, width)).reshape(owners, region, width)
    ranks = ranks_flat.reshape(owners, region)
    chosen = (ranks < counts[:, None])[..., None]
    new_resid = jnp.where(chosen, jnp.float32(0.0), accum).reshape(blocks, width)
    return (accum, ranks, chosen, new_resid)


def pack_slots(accum, ranks, counts, slots, region):
    order = lax.iota(jnp.int32, slots)
    picks = (ranks[:, None, :] == order[None, :, None]) & (
        order[None, :, None] < counts[:, None, None]
    )
    picks_f = picks.astype(jnp.float32)
    places = lax.iota(jnp.int32, region).astype(jnp.float32)
    packed = jnp.einsum("nkr,nrd->nkd", picks_f, accum, precision=lax.Precision.HIGHEST)
    where_at = jnp.einsum("nkr,r->nk", picks_f, places, precision=lax.Precision.HIGHEST)
    return (packed, where_at)


def unpack_slots(arrived, spots, region, width):
    places = lax.iota(jnp.int32, region).astype(jnp.float32)
    placed = (spots.reshape(-1)[:, None] == places[None, :]).astype(jnp.float32)
    return jnp.einsum(
        "mr,md->rd", placed, arrived.reshape(-1, width), precision=lax.Precision.HIGHEST
    )


def owner_section(pod_sum, oresid, ranks_out, count_out):
    owner_acc = pod_sum + oresid
    passed = (ranks_out < count_out)[:, None]
    outgoing = jnp.where(passed, owner_acc, jnp.float32(0.0))
    kept = jnp.where(passed, jnp.float32(0.0), owner_acc)
    return (outgoing, kept)


def per_device(acts, cotangent, residual, owner_residual, in_count, in_rank, out_count, out_rank):
    owners = lax.axis_size("inner")
    steps = acts.shape[1]
    tokens = acts.shape[2]
    rows = acts.shape[3]
    cols = cotangent.shape[3]
    blocks = residual.shape[1]
    width = residual.shape[2]
    region = blocks // owners
    slots = max(1, region // 2)
    scale = 1.0 / math.sqrt(tokens * owners)
    resid = residual[0]
    oresid = owner_residual[0]
    crosses = []
    packs = []
    spots_all = []
    for step in range(steps):
        grad = (
            jnp.einsum(
                "tr,tc->rc", acts[0, step], cotangent[0, step], preferred_element_type=jnp.float32
            )
            * scale
        )
        counts = in_count[0, step]
        accum, ranks, chosen, resid = select_blocks(
            resid, grad, in_rank[0, step], counts, owners, region, width
        )
        packed, where_at = pack_slots(accum, ranks, counts, slots, region)
        packs.append(packed)
        spots_all.append(where_at)
    arrived, spots = (
        lax.all_to_all(
            jnp.concatenate(packs, axis=1), "inner", split_axis=0, concat_axis=0, tiled=True
        ),
        lax.all_to_all(
            jnp.concatenate(spots_all, axis=1), "inner", split_axis=0, concat_axis=0, tiled=True
        ),
    )
    outgoings = []
    for step in range(steps):
        pod_sum = unpack_slots(
            arrived[:, step * slots : (step + 1) * slots],
            spots[:, step * slots : (step + 1) * slots],
            region,
            width,
        )
        outgoing, oresid = owner_section(pod_sum, oresid, out_rank[0, step], out_count[0, step])
        outgoings.append(outgoing)
    summed = lax.psum(jnp.stack(outgoings), "outer")
    for step in range(steps):
        crosses.append(summed[step])
    deltas = []
    for cross in crosses:
        delta = cross.astype(jnp.bfloat16)
        deltas.append(lax.all_gather(delta, "inner", axis=0, tiled=True))
    total = deltas[0].astype(jnp.float32)
    for later in deltas[1:]:
        total = total + later.astype(jnp.float32)
    applied = (-step_size * total).astype(jnp.bfloat16)
    return (applied.reshape(rows, cols), resid[None], oresid[None])


def solution(mesh):
    return jax.shard_map(
        per_device,
        mesh=mesh,
        in_specs=(
            P(("outer", "inner"), None, None, None),
            P(("outer", "inner"), None, None, None),
            P(("outer", "inner"), None, None),
            P(("outer", "inner"), None, None),
            P(("outer", "inner"), None, None),
            P(("outer", "inner"), None, None),
            P(("outer", "inner"), None),
            P(("outer", "inner"), None, None),
        ),
        out_specs=(P(), P(("outer", "inner"), None, None), P(("outer", "inner"), None, None)),
        check_vma=False,
    )
```

profile of v0, /device:TPU:0, one launch (start us, length us, event | category | flops | bytes accessed | tf_op | source)
XLA Modules:
  0.0 107.5 jit_solution(2119383466452367216)
XLA Ops:
  0.6 0.0 copy-start.8
  0.6 0.0 copy-start.9
  0.7 0.6 copy-done.8
  1.3 0.8 slice_reduce_fusion.1
  2.2 0.1 iota_compare_fusion.2
  2.3 0.6 fusion.6
  2.9 0.6 fusion.10
  3.5 0.6 all_to_all.11
  4.1 6.4 %all-to-all-start = ((f32[8,1,256]{2,1,0:T(1,128)}), f32[8,1,256]{2,1,0:T(1,128)S(1)}, u32[]{:S(2)}, u32[]{:S(2)}) async-start(f32[8,1,256]{2,1,0:T(1,128)} %all_to_all.11), calls=%async_computation | async-start | bytes 16384 | tf_op jit(solution)/shard_map/all_to_all | solution.py:81
  10.5 0.1 broadcast_compare_fusion
  10.6 0.0 copy-done.9
  10.6 1.6 %convolution_multiply_fusion = f32[512,512]{1,0:T(8,128)S(1)} fusion(bf16[1,2,512,512]{3,2,1,0:T(8,128)(2,1)S(1)} %copy-done.9, bf16[1,2,512,512]{3,2,1,0:T(8,128)(2,1)} %param.8), kind=kOutput, calls=%fused_computation | convolution fusion | flops 268697600 | bytes 2097152 | tf_op jit(solution)/shard_map/tr,tc->rc/dot_general | solution.py:65
  12.2 0.0 copy-done.10
  12.2 0.0 copy-start.1
  12.2 0.5 convolution_multiply_fusion.1
  12.7 0.0 copy-start.2
  12.7 1.0 copy-done.2
  13.7 0.1 reshape.167
  13.7 0.0 copy-done.1
  13.7 0.0 copy-start
  13.8 1.0 reshape.168
  14.8 0.6 copy-done
  15.4 0.9 fusion.4
  16.3 0.3 copy-done.4
  16.6 1.6 %fusion = f32[8,128,128]{2,1,0:T(8,128)S(1)} fusion(f32[8,256,128]{2,1,0:T(8,128)S(1)} %copy-done.4, s32[8,256]{1,0:T(8,128)S(1)} %eq.64, pred[8,256]{1,0:T(8,128)(4,1)S(1)} %broadcast_compare_fusion, pred[8,128]{1,0:T(8,128)(4,1)S(1)} %get-tuple-element.23, f32[8,256,128]{2,1,0:T(8,128)S(1)} %bitcast.55, f32[8,256,128]{2,1,0:T(8,128)S(1)} %reshape.167), kind=kOutput, calls=%fused_computation.7 | convolution fusion | flops 403963904 | bytes 3681280 | tf_op jit(solution)/shard_map/nkr,nrd->nkd/dot_general | solution.py:26
  18.2 1.1 pad_maximum_fusion
  19.3 0.0 all-to-all-done
  19.3 5.2 %all-to-all-start.1 = ((f32[8,256,128]{2,1,0:T(8,128)}), f32[8,256,128]{2,1,0:T(8,128)}, u32[]{:S(2)}, u32[]{:S(2)}) async-start(f32[8,256,128]{2,1,0:T(8,128)} %pad_maximum_fusion), calls=%async_computation.1 | async-start | bytes 2097152 | tf_op jit(solution)/shard_map/all_to_all | solution.py:78
  24.5 0.1 reshape.172
  24.6 1.3 %reshape.173 = f32[1,2048,128]{2,1,0:T(8,128)S(1)} reshape(f32[512,512]{1,0:T(8,128)} %copy-done.1) | data formatting | bytes 2097152 | tf_op jit(solution)/shard_map/reshape | solution.py:12
  25.9 0.1 broadcast_bitcast_fusion
  26.0 0.0 copy-start.7
  26.0 0.6 copy-done.7
  26.7 0.6 fusion.41
  27.2 0.7 copy-done.6
  27.9 1.3 %compare_reduce_fusion = (pred[256]{0:T(512)(128)(4,1)S(1)}, pred[256]{0:T(512)(128)(4,1)S(1)}) fusion(s32[1,2,256]{2,1,0:T(2,128)S(1)} %copy-done.6, s32[]{:T(128)} %bitcast.18, s32[]{:T(128)} %bitcast), kind=kLoop, calls=%fused_computation.56 | loop fusion | flops 512 | bytes 2568 | tf_op jit(solution)/shard_map/lt | solution.py:41
  29.2 2.4 %add_select_fusion = f32[1,2048,128]{2,1,0:T(8,128)} fusion(f32[1,2048,128]{2,1,0:T(8,128)S(1)} %reshape.173, f32[1,2048,128]{2,1,0:T(8,128)S(1)} %copy-done, f32[1,2048,128]{2,1,0:T(8,128)S(1)} %reshape.172, pred[2048]{0:T(1024)(128)(4,1)S(1)} %lt.117, pred[2048]{0:T(1024)(128)(4,1)S(1)} %lt.115), kind=kLoop, calls=%fused_computation.6 | loop fusion | flops 1048576 | bytes 4198400 | tf_op jit(solution)/shard_map/jit(_where)/select_n | solution.py:15
  31.7 19.5 %all-to-all-done.1 = f32[8,256,128]{2,1,0:T(8,128)} async-done(((f32[8,256,128]{2,1,0:T(8,128)}), f32[8,256,128]{2,1,0:T(8,128)}, u32[]{:S(2)}, u32[]{:S(2)}) %all-to-all-start.1) | async-done | bytes 1048608 | tf_op jit(solution)/shard_map/all_to_all | solution.py:78
  51.2 1.3 %fusion.39 = (f32[8,128,128]{2,1,0:T(8,128)S(1)}, f32[8,128,128]{2,1,0:T(8,128)S(1)}) fusion(f32[8,256,128]{2,1,0:T(8,128)} %all-to-all-done.1), kind=kLoop, calls=%fused_computation.64 | loop fusion | bytes 2097152 | tf_op jit(solution)/shard_map/slice | solution.py:88
  52.5 0.0 copy-done.5
  52.5 1.2 %convolution_add_fusion.1 = f32[256,128]{1,0:T(8,128)S(1)} fusion(f32[1024,128]{1,0:T(8,128)S(1)} %bitcast.57, f32[256]{0:T(256)S(1)} %iota_convert_fusion, f32[1024]{0:T(1024)S(1)} %get-tuple-element.15, f32[1,256,128]{2,1,0:T(8,128)S(1)} %copy-done.5), kind=kOutput, calls=%fused_computation.3 | convolution fusion | flops 402948096 | bytes 791552 | tf_op jit(solution)/shard_map/mr,md->rd/dot_general | solution.py:34
  53.7 0.1 select_bitcast_fusion.2
  53.8 1.8 %select_bitcast_fusion = (f32[1,256,128]{2,1,0:T(8,128)}, f32[1,256,128]{2,1,0:T(8,128)S(1)}) fusion(pred[256]{0:T(512)(128)(4,1)S(1)} %get-tuple-element.5, f32[256,128]{1,0:T(8,128)S(1)} %convolution_add_fusion.1, pred[256]{0:T(512)(128)(4,1)S(1)} %get-tuple-element.6, f32[1024,128]{1,0:T(8,128)S(1)} %bitcast.56, f32[256]{0:T(256)S(1)} %iota_convert_fusion, ...), kind=kOutput, calls=%fused_computation.44 | convolution fusion | flops 403046400 | bytes 923136 | tf_op jit(solution)/shard_map/mr,md->rd/dot_general | solution.py:34
  55.6 20.9 %all-reduce.1 = bf16[2,256,128]{2,1,0:T(8,128)(2,1)S(1)} all-reduce(f32[2,256,128]{2,1,0:T(8,128)S(1)} %pad_maximum_fusion.1), channel_id=1, replica_groups=mesh['outer'=4,'inner'=8] {'outer'}, use_global_device_ids=true, to_apply=%region_0.1 | all-reduce | flops 65536 | bytes 393216 | tf_op jit(solution)/shard_map/psum | solution.py:95
  76.5 14.8 %all-gather = bf16[1,2048,128]{2,1,0:T(8,128)(2,1)S(1)} all-gather(bf16[1,256,128]{2,1,0:T(8,128)(2,1)S(1)} %get-tuple-element.11), channel_id=2, replica_groups=mesh['outer'=4,'inner'=8] {'inner'}, dimensions={1}, use_global_device_ids=true | all-gather | bytes 589824 | tf_op jit(solution)/shard_map/all_gather | solution.py:101
  91.4 14.8 %all-gather.1 = bf16[1,2048,128]{2,1,0:T(8,128)(2,1)S(1)} all-gather(bf16[1,256,128]{2,1,0:T(8,128)(2,1)S(1)} %get-tuple-element.12), channel_id=3, replica_groups=mesh['outer'=4,'inner'=8] {'inner'}, dimensions={1}, use_global_device_ids=true | all-gather | bytes 589824 | tf_op jit(solution)/shard_map/all_gather | solution.py:101
  106.2 0.2 multiply_convert_fusion
  106.4 1.1 %reshape.171 = bf16[512,512]{1,0:T(8,128)(2,1)} reshape(bf16[1,2048,128]{2,1,0:T(8,128)(2,1)S(1)} %multiply_convert_fusion) | data formatting | bytes 1048576 | tf_op jit(solution)/shard_map/reshape | solution.py:106
  (19 shorter events, 0.1 us)
Async XLA Ops:
  0.6 0.7 copy-start.8
  0.6 9.9 %copy-start.9 = (bf16[1,2,512,512]{3,2,1,0:T(8,128)(2,1)S(1)}, bf16[1,2,512,512]{3,2,1,0:T(8,128)(2,1)}, u32[]{:S(2)}) copy-start(bf16[1,2,512,512]{3,2,1,0:T(8,128)(2,1)} %param.9) | copy-start | bytes 3145732
  4.1 15.1 %all-to-all-start = ((f32[8,1,256]{2,1,0:T(1,128)}), f32[8,1,256]{2,1,0:T(1,128)S(1)}, u32[]{:S(2)}, u32[]{:S(2)}) async-start(f32[8,1,256]{2,1,0:T(1,128)} %all_to_all.11), calls=%async_computation | async-start | bytes 16384 | tf_op jit(solution)/shard_map/all_to_all | solution.py:81
  10.6 1.6 %copy-start.10 = (bf16[1,2,512,512]{3,2,1,0:T(8,128)(2,1)S(1)}, bf16[1,2,512,512]{3,2,1,0:T(8,128)(2,1)}, u32[]{:S(2)}) copy-start(bf16[1,2,512,512]{3,2,1,0:T(8,128)(2,1)} %param.8) | copy-start | bytes 3145732
  12.2 1.6 %copy-start.1 = (f32[512,512]{1,0:T(8,128)}, f32[512,512]{1,0:T(8,128)S(1)}, u32[]{:S(2)}) copy-start(f32[512,512]{1,0:T(8,128)S(1)} %convolution_multiply_fusion) | copy-start | bytes 3145732
  12.7 1.0 copy-start.2
  13.7 1.6 %copy-start = (f32[1,2048,128]{2,1,0:T(8,128)S(1)}, f32[1,2048,128]{2,1,0:T(8,128)}, u32[]{:S(2)}) copy-start(f32[1,2048,128]{2,1,0:T(8,128)} %param.10) | copy-start | bytes 3145732
  15.4 1.2 %copy-start.4 = (f32[8,256,128]{2,1,0:T(8,128)S(1)}, f32[8,256,128]{2,1,0:T(8,128)}, u32[]{:S(2)}) copy-start(f32[8,256,128]{2,1,0:T(8,128)} %reshape.168) | copy-start | bytes 3145732
  19.3 5.2 %copy-start.3 = (f32[512,512]{1,0:T(8,128)S(1)}, f32[512,512]{1,0:T(8,128)}, u32[]{:S(2)}) copy-start(f32[512,512]{1,0:T(8,128)} %copy-done.2) | copy-start | bytes 3145732
  19.3 31.9 %all-to-all-start.1 = ((f32[8,256,128]{2,1,0:T(8,128)}), f32[8,256,128]{2,1,0:T(8,128)}, u32[]{:S(2)}, u32[]{:S(2)}) async-start(f32[8,256,128]{2,1,0:T(8,128)} %pad_maximum_fusion), calls=%async_computation.1 | async-start | bytes 2097152 | tf_op jit(solution)/shard_map/all_to_all | solution.py:78
  26.0 0.7 copy-start.7
  27.2 0.7 copy-start.6
  31.7 20.8 %copy-start.5 = (f32[1,256,128]{2,1,0:T(8,128)S(1)}, f32[1,256,128]{2,1,0:T(8,128)}, u32[]{:S(2)}) copy-start(f32[1,256,128]{2,1,0:T(8,128)} %param.11) | copy-start | bytes 393220
where the time goes:
time: 108 us; the launch traced here: 107 us
  blocking collectives  50.6 us (47%)
  waiting for transfers between devices  19.5 us (18%)
  starting transfers between devices  11.6 us (11%)
  local copies, waits for them, and re-layouts  10.9 us (10%)
  matrix products  8.8 us (8%)
  other arithmetic  5.26 us (5%)
    all_gather x2, blocking collectives, per_device(): deltas.append(lax.all_gather(delta, 'inner', axis=0, tiled=True))  29.6 us
    psum x1, blocking collectives, per_device(): summed = lax.psum(jnp.stack(outgoings), 'outer')  20.9 us
    all_to_all x1, waiting for transfers between devices, per_device(): lax.all_to_all(jnp.concatenate(packs, axis=1), 'inner', split_axis=0, con...  19.5 us
    all_to_all x1, starting transfers between devices, per_device(): lax.all_to_all(jnp.concatenate(spots_all, axis=1), 'inner', split_axis=0,...  6.35 us
    all_to_all x1, starting transfers between devices, per_device(): lax.all_to_all(jnp.concatenate(packs, axis=1), 'inner', split_axis=0, con...  5.23 us
    unnamed x26, local copies, waits for them, and re-layouts  3.94 us
    dot_general x2, matrix products, unpack_slots(): jnp.einsum('mr,md->rd', placed, arrived.reshape(-1, width), precision=lax...  2.97 us
    dot_general x2, matrix products, pack_slots(): jnp.einsum('nkr,nrd->nkd', picks_f, accum, precision=lax.Precision.HIGHEST)  2.51 us
  transfers between devices with their start and end apart: 2, of which 1 were waited for; matrix products, arithmetic and copies ran while one was open for 12% of the time, Pallas kernels for 0%

commit v1 on v0

--- a/solution.py
+++ b/solution.py
@@ -92,7 +92,9 @@
         )
         outgoing, oresid = owner_section(pod_sum, oresid, out_rank[0, step], out_count[0, step])
         outgoings.append(outgoing)
-    summed = lax.psum(jnp.stack(outgoings), "outer")
+    tile_in = jnp.stack(outgoings)
+    shaped = jax.lax.all_gather(tile_in, "outer")
+    summed = jnp.sum(shaped, 0)
     for step in range(steps):
         crosses.append(summed[step])
     deltas = []

time: 108 us -> 127 us (1.18)
  waiting for transfers between devices: 19.5 us -> 45.6 us
  blocking collectives: 50.6 us -> 29.5 us
  between operations: 0.85 us -> 14.3 us
  other arithmetic: 5.26 us -> 7.23 us
  local copies, waits for them, and re-layouts: 10.9 us -> 9.02 us
    all_gather x0 -> x1, waiting for transfers between devices: none -> 21.7 us  [per_device(): shaped = jax.lax.all_gather(tile_in, 'outer')]
    psum x1 -> x0, blocking collectives: 20.9 us -> none  [per_device(): summed = lax.psum(jnp.stack(outgoings), 'outer')]
    all_to_all x1, waiting for transfers between devices: 19.5 us -> 23.9 us  [per_device(): lax.all_to_all(jnp.concatenate(packs, axis=1), 'inner', split_axis=0, con...]
    reduce_sum x0 -> x1, other arithmetic: none -> 1.29 us  [per_device(): summed = jnp.sum(shaped, 0)]
  transfers between devices with their start and end apart: 2 -> 3, of which waited for: 1 -> 2; matrix products, arithmetic and copies ran while one was open for 12% -> 10% of each run, Pallas kernels for 0% -> 0%
where the time goes in v1:
time: 127 us; the launch traced here: 126 us
  waiting for transfers between devices  45.6 us (36%)
  blocking collectives  29.5 us (23%)
  between operations  14.3 us (11%)
  starting transfers between devices  11.6 us (9%)
  local copies, waits for them, and re-layouts  9.02 us (7%)
  matrix products  8.8 us (7%)
  other arithmetic  7.23 us (6%)
    all_gather x2, blocking collectives, per_device(): deltas.append(lax.all_gather(delta, 'inner', axis=0, tiled=True))  29.5 us
    all_to_all x1, waiting for transfers between devices, per_device(): lax.all_to_all(jnp.concatenate(packs, axis=1), 'inner', split_axis=0, con...  23.9 us
    all_gather x1, waiting for transfers between devices, per_device(): shaped = jax.lax.all_gather(tile_in, 'outer')  21.7 us
    all_to_all x1, starting transfers between devices, per_device(): lax.all_to_all(jnp.concatenate(spots_all, axis=1), 'inner', split_axis=0,...  6.35 us
    all_to_all x1, starting transfers between devices, per_device(): lax.all_to_all(jnp.concatenate(packs, axis=1), 'inner', split_axis=0, con...  5.23 us
    unnamed x26, local copies, waits for them, and re-layouts  3.29 us
    dot_general x2, matrix products, unpack_slots(): jnp.einsum('mr,md->rd', placed, arrived.reshape(-1, width), precision=lax...  2.97 us
  transfers between devices with their start and end apart: 3, of which 2 were waited for; matrix products, arithmetic and copies ran while one was open for 10% of the time, Pallas kernels for 0%

profile of v1, /device:TPU:0, one launch (start us, length us, event | category | flops | bytes accessed | tf_op | source)
XLA Modules:
  0.0 126.1 jit_solution(5945072694557828052)
XLA Ops:
  7.2 0.0 copy-start.8
  7.2 0.0 copy-start.9
  7.2 0.6 copy-done.8
  7.8 0.8 slice_reduce_fusion.1
  8.7 0.1 iota_compare_fusion.2
  8.8 0.6 fusion.6
  9.4 0.6 fusion.10
  10.1 0.6 all_to_all.11
  10.7 6.4 %all-to-all-start = ((f32[8,1,256]{2,1,0:T(1,128)}), f32[8,1,256]{2,1,0:T(1,128)S(1)}, u32[]{:S(2)}, u32[]{:S(2)}) async-start(f32[8,1,256]{2,1,0:T(1,128)} %all_to_all.11), calls=%async_computation | async-start | bytes 16384 | tf_op jit(solution)/shard_map/all_to_all | solution.py:81
  17.0 0.1 broadcast_compare_fusion
  17.1 0.0 copy-done.9
  17.1 1.6 %convolution_multiply_fusion = f32[512,512]{1,0:T(8,128)S(1)} fusion(bf16[1,2,512,512]{3,2,1,0:T(8,128)(2,1)S(1)} %copy-done.9, bf16[1,2,512,512]{3,2,1,0:T(8,128)(2,1)} %param.8), kind=kOutput, calls=%fused_computation | convolution fusion | flops 268697600 | bytes 2097152 | tf_op jit(solution)/shard_map/tr,tc->rc/dot_general | solution.py:65
  18.7 0.0 copy-done.10
  18.7 0.5 convolution_multiply_fusion.1
  19.2 0.0 copy-start.2
  19.2 1.0 copy-done.2
  20.2 0.1 reshape.167
  20.3 0.0 copy-start
  20.3 1.0 reshape.168
  21.3 0.6 copy-done
  21.9 0.9 fusion.4
  22.8 0.3 copy-done.4
  23.1 1.6 %fusion = f32[8,128,128]{2,1,0:T(8,128)S(1)} fusion(f32[8,256,128]{2,1,0:T(8,128)S(1)} %copy-done.4, s32[8,256]{1,0:T(8,128)S(1)} %eq.64, pred[8,256]{1,0:T(8,128)(4,1)S(1)} %broadcast_compare_fusion, pred[8,128]{1,0:T(8,128)(4,1)S(1)} %get-tuple-element.23, f32[8,256,128]{2,1,0:T(8,128)S(1)} %bitcast.56, f32[8,256,128]{2,1,0:T(8,128)S(1)} %reshape.167), kind=kOutput, calls=%fused_computation.7 | convolution fusion | flops 403963904 | bytes 3681280 | tf_op jit(solution)/shard_map/nkr,nrd->nkd/dot_general | solution.py:26
  24.7 1.0 pad_maximum_fusion
  25.8 0.0 all-to-all-done
  25.8 5.2 %all-to-all-start.1 = ((f32[8,256,128]{2,1,0:T(8,128)}), f32[8,256,128]{2,1,0:T(8,128)S(1)}, u32[]{:S(2)}, u32[]{:S(2)}) async-start(f32[8,256,128]{2,1,0:T(8,128)} %pad_maximum_fusion), calls=%async_computation.1 | async-start | bytes 2097152 | tf_op jit(solution)/shard_map/all_to_all | solution.py:78
  31.0 0.0 all-gather.5.cloned.1.call-start
  31.1 0.6 fusion.41
  31.7 0.7 copy-done.6
  32.3 1.3 %compare_reduce_fusion = (pred[256]{0:T(512)(128)(4,1)S(1)}, pred[256]{0:T(512)(128)(4,1)S(1)}) fusion(s32[1,2,256]{2,1,0:T(2,128)S(1)} %copy-done.6, s32[]{:T(128)} %bitcast.18, s32[]{:T(128)} %bitcast), kind=kLoop, calls=%fused_computation.56 | loop fusion | flops 512 | bytes 2568 | tf_op jit(solution)/shard_map/lt | solution.py:41
  33.7 0.0 copy-start.5
  33.7 23.9 %all-to-all-done.1 = f32[8,256,128]{2,1,0:T(8,128)S(1)} async-done(((f32[8,256,128]{2,1,0:T(8,128)}), f32[8,256,128]{2,1,0:T(8,128)S(1)}, u32[]{:S(2)}, u32[]{:S(2)}) %all-to-all-start.1) | async-done | bytes 1048608 | tf_op jit(solution)/shard_map/all_to_all | solution.py:78
  57.6 0.1 fusion.39
  57.7 1.2 convolution_add_fusion.1
  58.8 0.1 select_bitcast_fusion.2
  58.9 1.8 %select_bitcast_fusion = (f32[1,256,128]{2,1,0:T(8,128)}, f32[1,256,128]{2,1,0:T(8,128)S(1)}) fusion(pred[256]{0:T(512)(128)(4,1)S(1)} %get-tuple-element.5, f32[256,128]{1,0:T(8,128)S(1)} %convolution_add_fusion.1, pred[256]{0:T(512)(128)(4,1)S(1)} %get-tuple-element.6, f32[1024,128]{1,0:T(8,128)S(1)} %bitcast.57, f32[256]{0:T(256)S(1)} %iota_convert_fusion, ...), kind=kOutput, calls=%fused_computation.44 | convolution fusion | flops 403046400 | bytes 923136 | tf_op jit(solution)/shard_map/mr,md->rd/dot_general | solution.py:34
  60.8 0.7 pad_maximum_fusion.1
  61.5 0.0 all-gather.5.cloned.1.call-update
  61.5 0.1 reshape.172
  61.6 1.3 %reshape.173 = f32[1,2048,128]{2,1,0:T(8,128)S(1)} reshape(f32[512,512]{1,0:T(8,128)} %copy-done.1) | data formatting | bytes 2097152 | tf_op jit(solution)/shard_map/reshape | solution.py:12
  62.9 0.1 broadcast_bitcast_fusion
  63.0 2.4 %add_select_fusion = f32[1,2048,128]{2,1,0:T(8,128)} fusion(f32[1,2048,128]{2,1,0:T(8,128)S(1)} %reshape.173, f32[1,2048,128]{2,1,0:T(8,128)S(1)} %copy-done, f32[1,2048,128]{2,1,0:T(8,128)S(1)} %reshape.172, pred[2048]{0:T(1024)(128)(4,1)S(1)} %lt.117, pred[2048]{0:T(1024)(128)(4,1)S(1)} %lt.115), kind=kLoop, calls=%fused_computation.6 | loop fusion | flops 1048576 | bytes 4198400 | tf_op jit(solution)/shard_map/jit(_where)/select_n | solution.py:15
  65.4 21.7 %all-gather.5.cloned.1.call-done = f32[8,256,128]{2,1,0:T(8,128)} async-done(((f32[2,256,128]{2,1,0:T(8,128)}), f32[8,256,128]{2,1,0:T(8,128)}) %all-gather.5.cloned.1.call-update) | async-done | bytes 1048592 | tf_op jit(solution)/shard_map/all_gather | solution.py:96
  87.1 1.3 %reduce_sum.9 = bf16[2,256,128]{2,1,0:T(8,128)(2,1)S(1)} reduce(f32[4,2,256,128]{3,2,1,0:T(8,128)} %bitcast.59, f32[]{:T(128)} %constant.1.clone.1), dimensions={0}, to_apply=%region_0.1 | reduce | flops 196608 | bytes 1179652 | tf_op jit(solution)/shard_map/reduce_sum | solution.py:97
  88.4 14.8 %all-gather.1 = bf16[1,2048,128]{2,1,0:T(8,128)(2,1)S(1)} all-gather(bf16[1,256,128]{2,1,0:T(8,128)(2,1)S(1)} %get-tuple-element.11), channel_id=3, replica_groups=mesh['outer'=4,'inner'=8] {'inner'}, dimensions={1}, use_global_device_ids=true | all-gather | bytes 589824 | tf_op jit(solution)/shard_map/all_gather | solution.py:103
  103.2 14.8 %all-gather.2 = bf16[1,2048,128]{2,1,0:T(8,128)(2,1)S(1)} all-gather(bf16[1,256,128]{2,1,0:T(8,128)(2,1)S(1)} %get-tuple-element.12), channel_id=4, replica_groups=mesh['outer'=4,'inner'=8] {'inner'}, dimensions={1}, use_global_device_ids=true | all-gather | bytes 589824 | tf_op jit(solution)/shard_map/all_gather | solution.py:103
  118.0 0.2 multiply_convert_fusion
  118.1 1.1 reshape.171
  (22 shorter events, 0.1 us)
Async XLA Ops:
  7.2 0.7 copy-start.8
  7.2 9.9 %copy-start.9 = (bf16[1,2,512,512]{3,2,1,0:T(8,128)(2,1)S(1)}, bf16[1,2,512,512]{3,2,1,0:T(8,128)(2,1)}, u32[]{:S(2)}) copy-start(bf16[1,2,512,512]{3,2,1,0:T(8,128)(2,1)} %param.9) | copy-start | bytes 3145732
  10.7 15.1 %all-to-all-start = ((f32[8,1,256]{2,1,0:T(1,128)}), f32[8,1,256]{2,1,0:T(1,128)S(1)}, u32[]{:S(2)}, u32[]{:S(2)}) async-start(f32[8,1,256]{2,1,0:T(1,128)} %all_to_all.11), calls=%async_computation | async-start | bytes 16384 | tf_op jit(solution)/shard_map/all_to_all | solution.py:81
  17.1 1.6 %copy-start.10 = (bf16[1,2,512,512]{3,2,1,0:T(8,128)(2,1)S(1)}, bf16[1,2,512,512]{3,2,1,0:T(8,128)(2,1)}, u32[]{:S(2)}) copy-start(bf16[1,2,512,512]{3,2,1,0:T(8,128)(2,1)} %param.8) | copy-start | bytes 3145732
  18.7 1.5 %copy-start.1 = (f32[512,512]{1,0:T(8,128)}, f32[512,512]{1,0:T(8,128)S(1)}, u32[]{:S(2)}) copy-start(f32[512,512]{1,0:T(8,128)S(1)} %convolution_multiply_fusion) | copy-start | bytes 3145732
  19.2 1.0 copy-start.2
  20.3 1.6 %copy-start = (f32[1,2048,128]{2,1,0:T(8,128)S(1)}, f32[1,2048,128]{2,1,0:T(8,128)}, u32[]{:S(2)}) copy-start(f32[1,2048,128]{2,1,0:T(8,128)} %param.10) | copy-start | bytes 3145732
  21.9 1.2 copy-start.4
  25.8 5.3 %copy-start.7 = (s32[1,2]{1,0:T(1,128)S(1)}, s32[1,2]{1,0:T(1,128)}, u32[]{:S(2)}) copy-start(s32[1,2]{1,0:T(1,128)} %param.14) | copy-start | bytes 28
  25.8 31.8 %all-to-all-start.1 = ((f32[8,256,128]{2,1,0:T(8,128)}), f32[8,256,128]{2,1,0:T(8,128)S(1)}, u32[]{:S(2)}, u32[]{:S(2)}) async-start(f32[8,256,128]{2,1,0:T(8,128)} %pad_maximum_fusion), calls=%async_computation.1 | async-start | bytes 2097152 | tf_op jit(solution)/shard_map/all_to_all | solution.py:78
  31.0 56.1 %all-gather.5.cloned.1.call-start = ((), (), s32[]{:S(2)}) async-start(), calls=%async_computation.2 | async-start | bytes 1310720 | tf_op jit(solution)/shard_map/all_gather | solution.py:96
  31.6 0.7 copy-start.6
  33.7 24.0 %copy-start.5 = (f32[1,256,128]{2,1,0:T(8,128)S(1)}, f32[1,256,128]{2,1,0:T(8,128)}, u32[]{:S(2)}) copy-start(f32[1,256,128]{2,1,0:T(8,128)} %param.11) | copy-start | bytes 393220
  58.8 2.7 %copy-start.3 = (f32[512,512]{1,0:T(8,128)S(1)}, f32[512,512]{1,0:T(8,128)}, u32[]{:S(2)}) copy-start(f32[512,512]{1,0:T(8,128)} %copy-done.2) | copy-start | bytes 3145732
Sparse Core Ops, SparseCore 0:
  61.6 25.4 all-gather.4
